TPU v7x, 32 devices: a whole 2x2x4 slice. The times are simulated.
32 devices in a mesh: row: 8 (over y, x, core), col: 4 (over z).
Axes of the slice: x: 2, y: 2, z: 4, core: 2. Of those that a mesh axis runs over, the one named last changes fastest.
Arguments:
- temps: bfloat16 [12, 64, 16384], P(None, None, ('row', 'col')), may hold values from -6 to 6
- sensors: int32 [12, 512], replicated, may hold values from 0 to 16383
Outputs:
- corr: bfloat16 [512, 16384], P('col', 'row')
Inputs may be any that keep to these rules, and one draw needn't show every extreme that they name: `sensors`: each entry is a pixel index of its tier; candidates may repeat.
All inputs are finite; a program needn't handle non-finite values.
Results may differ from a plain program's by a relative error of at most 0.001.
Values may be sent and summed in bfloat16 or wider, within the bound.
A program may use at most 64 MiB of HBM per device.

v0:
```python
import jax
import jax.numpy as jnp
from jax import lax
from jax.sharding import PartitionSpec as P


def select_columns(fields, sensor_rows, first_pixel):
    width = fields.shape[2]
    offsets = sensor_rows - first_pixel
    pixel_ids = lax.broadcasted_iota(jnp.int32, (width, sensor_rows.shape[1]), 0)

    def one_tier(pair):
        tier_fields, tier_offsets = pair
        selector = (pixel_ids == tier_offsets[None, :]).astype(jnp.bfloat16)
        return jnp.dot(tier_fields, selector, preferred_element_type=jnp.float32)

    return lax.map(one_tier, (fields, offsets))


def body(temps, sensors):
    col_count = lax.axis_size("col")
    first_pixel = (lax.axis_index("row") * col_count + lax.axis_index("col")) * temps.shape[2]
    local_values = select_columns(temps, sensors, first_pixel)
    owned = lax.psum_scatter(
        local_values.astype(jnp.bfloat16), "col", scatter_dimension=2, tiled=True
    )
    readings = lax.psum(owned, "row").astype(jnp.float32).astype(jnp.bfloat16)
    scale_factor = 1.0 / jnp.sqrt(jnp.float32(temps.shape[0] * temps.shape[1]))
    summed = jnp.einsum(
        "tsc,tsp->cp",
        lax.all_gather(readings, "col", axis=2, tiled=True),
        temps,
        preferred_element_type=jnp.float32,
    )
    rounded = (summed * scale_factor).astype(jnp.bfloat16)
    return lax.all_to_all(rounded, "col", split_axis=0, concat_axis=1, tiled=True)


def solution(mesh):
    placed = (P(None, None, ("row", "col")), P())
    return jax.shard_map(
        body, mesh=mesh, in_specs=placed, out_specs=P("col", "row"), check_vma=False
    )
```

profile of v0, /device:TPU:0, one launch (start us, length us, event | category | flops | bytes accessed | tf_op | source)
XLA Modules:
  0.0 149.4 jit_solution(5405462871860880620)
XLA Ops:
  6.5 0.0 reduce-scatter.4.cloned.1.call-start
  6.5 0.8 broadcast_subtract_fusion
  7.3 14.2 %while.11 = (s32[]{:T(128)}, bf16[12,64,512]{2,1,0:T(8,128)(2,1)S(1)}, bf16[12,64,512]{2,1,0:T(8,128)(2,1)}, s32[12,512]{1,0:T(8,128)S(1)}, s32[]{:T(128)}) while((s32[]{:T(128)}, bf16[12,64,512]{2,1,0:T(8,128)(2,1)S(1)}, bf16[12,64,512]{2,1,0:T(8,128)(2,1)}, s32[12,512]{1,0:T(8,128)S(1)}, s32[]{:T(128)}) %tuple.21), condition=%wide.region_1.2_spmd.clone, body=%wide.region_0.1_spmd.clone.sunk | while | flops 33816576 | bytes 203849 | solution.py:17
  7.3 1.2 fusion.14
  8.5 1.2 fusion.14
  9.7 1.2 fusion.14
  10.9 1.2 fusion.14
  12.1 1.2 fusion.14
  13.2 1.2 fusion.14
  14.4 1.2 fusion.14
  15.6 1.2 fusion.14
  16.8 1.2 fusion.14
  18.0 1.2 fusion.14
  19.2 1.2 fusion.14
  20.4 1.2 fusion.14
  21.5 2.0 %copy.5 = bf16[12,64,512]{1,0,2:T(8,128)(2,1)S(1)} copy(bf16[12,64,512]{2,1,0:T(8,128)(2,1)S(1)} %get-tuple-element.32) | data formatting | bytes 1572864
  23.5 2.0 %reshape.4 = bf16[512,768]{1,0:T(8,128)(2,1)} reshape(bf16[512,12,64]{2,1,0:T(8,128)(2,1)S(1)} %bitcast.28) | data formatting | bytes 1572864
  25.6 0.0 copy-start
  25.6 0.0 reduce-scatter.4.cloned.1.call-update
  25.6 0.0 all-reduce.2.cloned.1.call-start
  25.7 26.0 %reduce-scatter.4.cloned.1.call-done = bf16[128,768]{1,0:T(8,128)(2,1)} async-done(((bf16[512,768]{1,0:T(8,128)(2,1)}), bf16[128,768]{1,0:T(8,128)(2,1)}) %reduce-scatter.4.cloned.1.call-update) | async-done | bytes 196624
  51.7 1.3 reshape.5
  52.9 1.0 copy.6
  54.0 0.0 all-reduce.2.cloned.1.call-update
  54.0 53.9 %all-reduce.2.cloned.1.call-done = bf16[12,64,128]{2,1,0:T(8,128)(2,1)} async-done(((bf16[12,64,128]{2,1,0:T(8,128)(2,1)}), bf16[12,64,128]{2,1,0:T(8,128)(2,1)}) %all-reduce.2.cloned.1.call-update) | async-done | bytes 196624 | tf_op jit(solution)/shard_map/psum | solution.py:27
  107.9 18.8 %all_gather.3 = bf16[12,64,512]{2,1,0:T(8,128)(2,1)S(1)} all-gather(bf16[12,64,128]{2,1,0:T(8,128)(2,1)} %all-reduce.2.cloned.1.call-done), channel_id=1, replica_groups=mesh['row'=8,'col'=4] {'col'}, dimensions={2}, use_global_device_ids=true | all-gather | bytes 983040 | tf_op jit(solution)/shard_map/all_gather | solution.py:31
  126.7 0.0 copy-done
  126.7 0.6 fusion.8
  127.3 14.4 %all_to_all.19 = bf16[4,128,512]{2,1,0:T(8,128)(2,1)S(1)} all-to-all(bf16[4,128,512]{2,1,0:T(8,128)(2,1)S(1)} %bitcast.31), channel_id=1, replica_groups=mesh['row'=8,'col'=4] {'col'}, dimensions={0} | all-to-all | bytes 1048576 | tf_op jit(solution)/shard_map/all_to_all | solution.py:36
  141.8 0.8 copy.7
  (13 shorter events, 0.1 us)
Async XLA Ops:
  6.5 45.1 %reduce-scatter.4.cloned.1.call-start = ((), (), s32[]{:S(2)}) async-start(), calls=%async_computation.3 | async-start | bytes 983040
  25.6 101.2 %copy-start = (bf16[12,64,512]{2,1,0:T(8,128)(2,1)S(1)}, bf16[12,64,512]{2,1,0:T(8,128)(2,1)}, u32[]{:S(2)}) copy-start(bf16[12,64,512]{2,1,0:T(8,128)(2,1)} %get-tuple-element.99) | copy-start | bytes 2359300
  25.6 82.3 %all-reduce.2.cloned.1.call-start = ((), (), s32[]{:S(2)}) async-start(), calls=%async_computation.2 | async-start | bytes 393216 | tf_op jit(solution)/shard_map/psum | solution.py:27
Sparse Core Ops, SparseCore 0:
  25.7 25.8 reduce-scatter.3
  54.7 53.1 all-reduce.1
where the time goes:
time: 150 us; the launch traced here: 149 us
  waiting for transfers between devices  80 us (53%)
  blocking collectives  33.2 us (22%)
  matrix products  14.5 us (10%)
  between operations  13.4 us (9%)
  local copies, waits for them, and re-layouts  7.3 us (5%)
    psum x1, waiting for transfers between devices, body(): readings = lax.psum(owned, 'row').astype(jnp.float32).astype(jnp.bfloat16)  53.9 us
    unnamed x3, waiting for transfers between devices  26 us
    all_gather x1, blocking collectives, body(): lax.all_gather(readings, 'col', axis=2, tiled=True)  18.8 us
    all_to_all x1, blocking collectives, body(): lax.all_to_all(rounded, 'col', split_axis=0, concat_axis=1, tiled=True)  14.4 us
    dot_general x12, matrix products, one_tier(): return jnp.dot(tier_fields, selector, preferred_element_type=jnp.float32)  13.9 us
    unnamed x6, local copies, waits for them, and re-layouts  6.33 us
  transfers between devices with their start and end apart: 2, of which 2 were waited for; matrix products, arithmetic and copies ran while one was open for 0% of the time, Pallas kernels for 0%

commit v1 on v0

v1 whole, which is shorter than its diff:
```python
import functools

import jax
import numpy as np
import jax.numpy as jnp
from jax import lax
from jax.experimental import pallas as pl
from jax.experimental.pallas import tpu as pltpu
from jax.sharding import PartitionSpec as P

SUB = 16
MESH = pl.DeviceIdType.MESH


def kernel(
    n_row, n_col, n_chunk, tiers,
    temps_ref, sens_ref, out_ref,
    sens_t, part, rs_buf, z_src, z_buf, full, out_buf,
    rs_send, rs_recv, z_send, z_recv, ag_send, ag_recv, o_send, o_recv,
):
    r = lax.axis_index("row")
    z = lax.axis_index("col")
    snaps, width = temps_ref.shape[0] // tiers, temps_ref.shape[1]
    depth = temps_ref.shape[0]
    rows_col = out_ref.shape[0] // n_chunk
    rows_chunk = n_row * SUB
    scale = float(np.float32(1.0) / np.sqrt(np.float32(depth)))

    def row_peer(d):
        return lax.rem(r + d, n_row)

    def col_peer(e):
        return lax.rem(z + e, n_col)

    barrier = pltpu.get_barrier_semaphore()
    for d in range(1, n_row):
        pl.semaphore_signal(barrier, inc=1, device_id=(row_peer(d), z), device_id_type=MESH)
    for e in range(1, n_col):
        pl.semaphore_signal(barrier, inc=1, device_id=(r, col_peer(e)), device_id_type=MESH)

    first_pixel = (r * n_col + z) * width
    offsets = jnp.transpose(sens_ref[...] - first_pixel)
    sens_t[...] = offsets.reshape(sens_t.shape)
    pixel_ids = lax.broadcasted_iota(jnp.int32, (rows_chunk, width), 1)

    def select(k):
        mine = sens_t[:, k].reshape(rows_chunk, tiers)
        for t in range(0, tiers, 2):
            pair = []
            for u in (t, t + 1):
                hot = (pixel_ids == mine[:, u:u + 1]).astype(jnp.float32).astype(jnp.bfloat16)
                pair.append(lax.dot_general(
                    hot, temps_ref[u * snaps:(u + 1) * snaps, :],
                    (((1,), (1,)), ((), ())), preferred_element_type=jnp.float32,
                ))
            both = jnp.concatenate(pair, axis=1).astype(jnp.bfloat16)
            part[k, :, :, t * snaps:(t + 2) * snaps] = both.reshape(n_row, SUB, 2 * snaps)

    def start_rs(k):
        for d in range(1, n_row):
            peer = row_peer(d)
            pltpu.make_async_remote_copy(
                part.at[k, peer], rs_buf.at[k, d - 1], rs_send.at[k], rs_recv.at[k],
                device_id=(peer, z), device_id_type=MESH,
            ).start()

    def wait_all(ref, sem):
        pltpu.make_async_copy(ref, ref, sem).wait()

    def start_z(k):
        wait_all(rs_buf.at[k], rs_recv.at[k])
        total = part[k, r]
        for d in range(n_row - 1):
            total = total + rs_buf[k, d]
        z_src[k] = total
        for e in range(1, n_col):
            pltpu.make_async_remote_copy(
                z_src.at[k], z_buf.at[k, e - 1], z_send.at[k], z_recv.at[k],
                device_id=(r, col_peer(e)), device_id_type=MESH,
            ).start()

    def start_ag(k):
        wait_all(z_buf.at[k], z_recv.at[k])
        total = z_src[k]
        for e in range(n_col - 1):
            total = total + z_buf[k, e]
        full[k, r] = total
        for d in range(1, n_row):
            pltpu.make_async_remote_copy(
                full.at[k, r], full.at[k, r], ag_send.at[k], ag_recv.at[k],
                device_id=(row_peer(d), z), device_id_type=MESH,
            ).start()

    def start_out(k):
        wait_all(full.at[k, pl.ds(0, n_row - 1)], ag_recv.at[k])
        readings = full[k].reshape(rows_chunk, depth)
        summed = jnp.dot(readings, temps_ref[...], preferred_element_type=jnp.float32)
        out_buf[k] = (summed * scale).astype(jnp.bfloat16).reshape(n_col, rows_col, width)
        columns = pl.ds(pl.multiple_of(z * width, width), width)
        for e in range(1, n_col):
            peer = col_peer(e)
            pltpu.make_async_remote_copy(
                out_buf.at[k, peer], out_ref.at[pl.ds(k * rows_col, rows_col), columns],
                o_send.at[k], o_recv.at[k],
                device_id=(r, peer), device_id_type=MESH,
            ).start()
        out_ref[pl.ds(k * rows_col, rows_col), columns] = out_buf[k, z]

    select(0)
    pl.semaphore_wait(barrier, n_row + n_col - 2)
    start_rs(0)
    for k in range(1, n_chunk):
        select(k)
        start_rs(k)
    for step in range(n_chunk + 2):
        if step < n_chunk:
            start_z(step)
        if 0 <= step - 1 < n_chunk:
            start_ag(step - 1)
        if 0 <= step - 2 < n_chunk:
            start_out(step - 2)
    for k in range(n_chunk):
        wait_all(out_buf.at[k, pl.ds(0, n_col - 1)], o_recv.at[k])
        wait_all(rs_buf.at[k], rs_send.at[k])
        wait_all(z_buf.at[k], z_send.at[k])
        wait_all(full.at[k, pl.ds(0, n_row - 1)], ag_send.at[k])
        wait_all(out_buf.at[k, pl.ds(0, n_col - 1)], o_send.at[k])


def body(n_row, n_col, temps, sensors):
    tiers, snaps, width = temps.shape
    sens = sensors.shape[1]
    depth = tiers * snaps
    n_chunk = sens // (SUB * n_row)
    rows_out = sens // n_col
    rows_col = rows_out // n_chunk
    bf16 = jnp.bfloat16
    return pl.pallas_call(
        functools.partial(kernel, n_row, n_col, n_chunk, tiers),
        out_shape=jax.ShapeDtypeStruct((rows_out, n_col * width), bf16),
        in_specs=[pl.BlockSpec(memory_space=pltpu.VMEM)] * 2,
        out_specs=pl.BlockSpec(memory_space=pltpu.VMEM),
        scratch_shapes=[
            pltpu.VMEM((n_col, n_chunk, rows_col, tiers), jnp.int32),
            pltpu.VMEM((n_chunk, n_row, SUB, depth), bf16),
            pltpu.VMEM((n_chunk, n_row - 1, SUB, depth), bf16),
            pltpu.VMEM((n_chunk, SUB, depth), bf16),
            pltpu.VMEM((n_chunk, n_col - 1, SUB, depth), bf16),
            pltpu.VMEM((n_chunk, n_row, SUB, depth), bf16),
            pltpu.VMEM((n_chunk, n_col, rows_col, width), bf16),
        ] + [pltpu.SemaphoreType.DMA((n_chunk,))] * 8,
        compiler_params=pltpu.CompilerParams(collective_id=0, has_side_effects=True),
    )(temps.reshape(depth, width), sensors)


def solution(mesh):
    placed = (P(None, None, ("row", "col")), P())
    return jax.shard_map(
        functools.partial(body, mesh.shape["row"], mesh.shape["col"]),
        mesh=mesh, in_specs=placed, out_specs=P("col", "row"), check_vma=False,
    )
```

time: 150 us -> 39.8 us (0.27)
  waiting for transfers between devices: 80 us -> 0 us
  Pallas kernels: 0 us -> 37.7 us
  blocking collectives: 33.2 us -> 0 us
  matrix products: 14.5 us -> 0 us
  between operations: 13.4 us -> 0.01 us
  local copies, waits for them, and re-layouts: 7.3 us -> 1.88 us
    psum x1 -> x0, waiting for transfers between devices: 53.9 us -> none  [body(): readings = lax.psum(owned, 'row').astype(jnp.float32).astype(jnp.bfloat16)]
    pallas_call x0 -> x1, Pallas kernels: none -> 37.7 us  [body(): pl.pallas_call(functools.partial(kernel, n_row, n_col, n_chunk, tiers), o...]
    unnamed x3 -> x0, waiting for transfers between devices: 26 us -> none
    all_gather x1 -> x0, blocking collectives: 18.8 us -> none  [body(): lax.all_gather(readings, 'col', axis=2, tiled=True)]
    dot_general x13 -> x0, matrix products: 14.5 us -> none  [the longest x12 13.9 us: one_tier(): return jnp.dot(tier_fields, selector, preferred_element_type=jnp.float32)]
    all_to_all x1 -> x0, blocking collectives: 14.4 us -> none  [body(): lax.all_to_all(rounded, 'col', split_axis=0, concat_axis=1, tiled=True)]
    unnamed x6 -> x1, local copies, waits for them, and re-layouts: 6.33 us -> 1.88 us
  transfers between devices with their start and end apart: 2 -> 0, of which waited for: 2 -> 0; matrix products, arithmetic and copies ran while one was open for 0% -> 0% of each run, Pallas kernels for 0% -> 0%
where the time goes in v1:
time: 39.8 us; the launch traced here: 39.6 us
  Pallas kernels  37.7 us (95%)
  local copies, waits for them, and re-layouts  1.88 us (5%)
    pallas_call x1, Pallas kernels, body(): pl.pallas_call(functools.partial(kernel, n_row, n_col, n_chunk, tiers), o...  37.7 us
    unnamed x1, local copies, waits for them, and re-layouts  1.88 us

profile of v1, /device:TPU:0, one launch (start us, length us, event | category | flops | bytes accessed | tf_op | source)
XLA Modules:
  0.0 39.6 jit_solution(8997394981124526333)
XLA Ops:
  0.0 37.7 %shard_map.28 = bf16[128,2048]{1,0:T(8,128)(2,1)} custom-call(bf16[768,512]{1,0:T(8,128)(2,1)} %bitcast.1, s32[12,512]{1,0:T(8,128)} %sens_ref.1), custom_call_target="tpu_custom_call" | custom-call | tf_op jit(solution)/shard_map/pallas_call | solution.py:138
  37.7 1.9 %copy.4 = bf16[128,2048]{1,0:T(8,128)(2,1)} copy(bf16[128,2048]{1,0:T(8,128)(2,1)} %shard_map.28) | data formatting | bytes 1048576

commit v2 on v1

v2 whole, which is shorter than its diff:
```python
import functools

import jax
import numpy as np
import jax.numpy as jnp
from jax import lax
from jax.experimental import pallas as pl
from jax.experimental.pallas import tpu as pltpu
from jax.sharding import PartitionSpec as P

SUB = 16
MESH = pl.DeviceIdType.MESH


def kernel(
    n_row, n_col, n_chunk, tiers,
    temps_hbm, sens_ref, out_ref,
    temps_ref, sens_t, part, core_buf, pair_sum, rs_buf, z_src, z_buf, full, out_buf,
    c_send, c_recv, rs_send, rs_recv, z_send, z_recv,
    ag_send, ag_recv, d_send, d_recv, o_send, o_recv, t_sem,
):
    r = lax.axis_index("row")
    z = lax.axis_index("col")
    core, chip = lax.rem(r, 2), r // 2
    other = 1 - core
    n_chip = n_row // 2
    snaps, width = temps_ref.shape[0] // tiers, temps_ref.shape[1]
    depth = temps_ref.shape[0]
    rows_col = out_ref.shape[0] // n_chunk
    half = rows_col // 2
    rows_half = n_chip * SUB
    scale = float(np.float32(1.0) / np.sqrt(np.float32(depth)))
    partner = (chip * 2 + other, z)

    def chip_peer(d):
        peer = lax.rem(chip + d, n_chip)
        return peer, (peer * 2 + core, z)

    n_half = n_col // 2
    side = z // n_half

    def col_peer(e):
        return lax.rem(z + e, n_col)

    def out_peer(e):
        across = (1 - side) * n_half + lax.rem(z + e, n_half)
        beside = side * n_half + lax.rem(z + e, n_half)
        return across if e < n_half else beside

    load = pltpu.make_async_copy(temps_hbm, temps_ref, t_sem)
    load.start()
    barrier = pltpu.get_barrier_semaphore()
    pl.semaphore_signal(barrier, inc=1, device_id=partner, device_id_type=MESH)
    for d in range(1, n_chip):
        pl.semaphore_signal(barrier, inc=1, device_id=chip_peer(d)[1], device_id_type=MESH)
    for e in range(1, n_col):
        pl.semaphore_signal(barrier, inc=1, device_id=(r, col_peer(e)), device_id_type=MESH)

    first_pixel = (r * n_col + z) * width
    offsets = jnp.transpose(sens_ref[...] - first_pixel)
    sens_t[...] = offsets.reshape(sens_t.shape)
    pixel_ids = lax.broadcasted_iota(jnp.int32, (rows_half, width), 1)

    def wait_all(ref, sem):
        pltpu.make_async_copy(ref, ref, sem).wait()

    def select(k):
        for h in range(2):
            mine = sens_t[:, k, h].reshape(rows_half, tiers)
            for t in range(0, tiers, 2):
                pair = []
                for u in (t, t + 1):
                    hot = (pixel_ids == mine[:, u:u + 1]).astype(jnp.float32).astype(jnp.bfloat16)
                    pair.append(lax.dot_general(
                        hot, temps_ref[u * snaps:(u + 1) * snaps, :],
                        (((1,), (1,)), ((), ())), preferred_element_type=jnp.float32,
                    ))
                both = jnp.concatenate(pair, axis=1).astype(jnp.bfloat16)
                part[k, h, :, :, t * snaps:(t + 2) * snaps] = both.reshape(n_chip, SUB, 2 * snaps)

    def start_core(k):
        pltpu.make_async_remote_copy(
            part.at[k, other], core_buf.at[k], c_send.at[k], c_recv.at[k],
            device_id=partner, device_id_type=MESH,
        ).start()

    def start_rs(k):
        wait_all(core_buf.at[k], c_recv.at[k])
        pair_sum[k] = part[k, core] + core_buf[k]
        for d in range(1, n_chip):
            peer, device = chip_peer(d)
            pltpu.make_async_remote_copy(
                pair_sum.at[k, peer], rs_buf.at[k, d - 1], rs_send.at[k], rs_recv.at[k],
                device_id=device, device_id_type=MESH,
            ).start()

    def start_z(k):
        wait_all(rs_buf.at[k], rs_recv.at[k])
        total = pair_sum[k, chip]
        for d in range(n_chip - 1):
            total = total + rs_buf[k, d]
        z_src[k] = total
        for e in range(1, n_col):
            pltpu.make_async_remote_copy(
                z_src.at[k], z_buf.at[k, e - 1], z_send.at[k], z_recv.at[k],
                device_id=(r, col_peer(e)), device_id_type=MESH,
            ).start()

    def start_ag(k):
        wait_all(z_buf.at[k], z_recv.at[k])
        total = z_src[k]
        for e in range(n_col - 1):
            total = total + z_buf[k, e]
        full[k, core, chip] = total
        for d in range(1, n_chip):
            pltpu.make_async_remote_copy(
                full.at[k, core, chip], full.at[k, core, chip], ag_send.at[k], ag_recv.at[k],
                device_id=chip_peer(d)[1], device_id_type=MESH,
            ).start()

    def start_pass(k):
        wait_all(rs_buf.at[k], ag_recv.at[k])
        pltpu.make_async_remote_copy(
            full.at[k, core], full.at[k, core], d_send.at[k], d_recv.at[k],
            device_id=partner, device_id_type=MESH,
        ).start()

    def start_out(k):
        wait_all(core_buf.at[k], d_recv.at[k])
        readings = full[k].reshape(2 * rows_half, depth)
        summed = jnp.dot(readings, temps_ref[...], preferred_element_type=jnp.float32)
        rounded = (summed * scale).astype(jnp.bfloat16)
        for h in range(2):
            out_buf[k, :, h * half:(h + 1) * half] = rounded[h * rows_half:(h + 1) * rows_half].reshape(n_col, half, width)
        rows = pl.ds(k * rows_col, rows_col)
        columns = pl.ds(pl.multiple_of(z * width, width), width)
        for e in [*range(n_half), *range(n_half + 1, n_col)]:
            peer = out_peer(e)
            pltpu.make_async_remote_copy(
                out_buf.at[k, peer], out_ref.at[rows, columns], o_send.at[k], o_recv.at[k],
                device_id=(r, peer), device_id_type=MESH,
            ).start()
        out_ref[rows, columns] = out_buf[k, z]

    load.wait()
    select(0)
    pl.semaphore_wait(barrier, n_chip + n_col - 1)
    start_core(0)
    for k in range(1, n_chunk):
        select(k)
        start_core(k)
        start_rs(k - 1)
    start_rs(n_chunk - 1)
    stages = (start_z, start_ag, start_pass, start_out)
    due = [(at + 3.0 * k, late, k) for late, at in enumerate((0, 4.5, 8, 9.2)) for k in range(n_chunk)]
    for _, late, k in sorted(due):
        stages[late](k)
    for k in range(n_chunk):
        wait_all(out_buf.at[k, pl.ds(0, n_col - 1)], o_recv.at[k])
        wait_all(core_buf.at[k], c_send.at[k])
        wait_all(rs_buf.at[k], rs_send.at[k])
        wait_all(z_buf.at[k], z_send.at[k])
        wait_all(rs_buf.at[k], ag_send.at[k])
        wait_all(core_buf.at[k], d_send.at[k])
        wait_all(out_buf.at[k, pl.ds(0, n_col - 1)], o_send.at[k])


def body(n_row, n_col, temps, sensors):
    tiers, snaps, width = temps.shape
    sens = sensors.shape[1]
    depth = tiers * snaps
    n_chunk = sens // (SUB * n_row)
    n_chip = n_row // 2
    rows_out = sens // n_col
    rows_col = rows_out // n_chunk
    bf16 = jnp.bfloat16
    return pl.pallas_call(
        functools.partial(kernel, n_row, n_col, n_chunk, tiers),
        out_shape=pltpu.VMEM((rows_out, n_col * width), bf16),
        in_specs=[pl.BlockSpec(memory_space=pl.ANY), pl.BlockSpec(memory_space=pltpu.VMEM)],
        out_specs=pl.BlockSpec(memory_space=pltpu.VMEM),
        scratch_shapes=[
            pltpu.VMEM((depth, width), bf16),
            pltpu.VMEM((n_col, n_chunk, 2, rows_col // 2, tiers), jnp.int32),
            pltpu.VMEM((n_chunk, 2, n_chip, SUB, depth), bf16),
            pltpu.VMEM((n_chunk, n_chip, SUB, depth), bf16),
            pltpu.VMEM((n_chunk, n_chip, SUB, depth), bf16),
            pltpu.VMEM((n_chunk, n_chip - 1, SUB, depth), bf16),
            pltpu.VMEM((n_chunk, SUB, depth), bf16),
            pltpu.VMEM((n_chunk, n_col - 1, SUB, depth), bf16),
            pltpu.VMEM((n_chunk, 2, n_chip, SUB, depth), bf16),
            pltpu.VMEM((n_chunk, n_col, rows_col, width), bf16),
        ] + [pltpu.SemaphoreType.DMA((n_chunk,))] * 12 + [pltpu.SemaphoreType.DMA],
        compiler_params=pltpu.CompilerParams(collective_id=0, has_side_effects=True),
    )(temps.reshape(depth, width), sensors)


def solution(mesh):
    placed = (P(None, None, ("row", "col")), P())
    return jax.shard_map(
        functools.partial(body, mesh.shape["row"], mesh.shape["col"]),
        mesh=mesh, in_specs=placed, out_specs=P("col", "row"), check_vma=False,
    )
```

time: 39.8 us -> 34.3 us (0.86)
  Pallas kernels: 37.7 us -> 33.1 us
  local copies, waits for them, and re-layouts: 1.88 us -> 0.8 us
    pallas_call x1, Pallas kernels: 37.7 us -> 33.1 us  [body(): pl.pallas_call(functools.partial(kernel, n_row, n_col, n_chunk, tiers), o...]
    unnamed x1, local copies, waits for them, and re-layouts: 1.88 us -> 0.8 us
where the time goes in v2:
time: 34.3 us; the launch traced here: 33.9 us
  Pallas kernels  33.1 us (97%)
  local copies, waits for them, and re-layouts  0.8 us (2%)
    pallas_call x1, Pallas kernels, body(): pl.pallas_call(functools.partial(kernel, n_row, n_col, n_chunk, tiers), o...  33.1 us
    unnamed x1, local copies, waits for them, and re-layouts  0.8 us

profile of v2, /device:TPU:0, one launch (start us, length us, event | category | flops | bytes accessed | tf_op | source)
XLA Modules:
  0.0 33.9 jit_solution(398406487779118889)
XLA Ops:
  0.0 33.1 %shard_map.28 = bf16[128,2048]{1,0:T(8,128)(2,1)S(1)} custom-call(bf16[768,512]{1,0:T(8,128)(2,1)} %bitcast.1, s32[12,512]{1,0:T(8,128)} %sens_ref.1), custom_call_target="tpu_custom_call" | custom-call | tf_op jit(solution)/shard_map/pallas_call | solution.py:177
  33.1 0.8 %copy.4 = bf16[128,2048]{1,0:T(8,128)(2,1)} copy(bf16[128,2048]{1,0:T(8,128)(2,1)S(1)} %shard_map.28) | data formatting | bytes 1048576
